TPU v7x, 256 devices: a whole 4x4x8 slice. The times are simulated.
256 devices in a mesh: chol: 32 (over z_hi, y, x), virt: 8 (over z_lo, core).
Axes of the slice: x: 4, y: 4, z: 8 (z_hi: 2, z_lo: 4; z = z_hi * 4 + z_lo), core: 2. Of those that a mesh axis runs over, the one named last changes fastest.
Arguments:
- amplitudes: bfloat16 [9600, 600], P('chol'), may hold values from -6 to 6
- chol_vectors: bfloat16 [256, 600, 600], P('chol', 'virt'), may hold values from -0.061035156 to 0.061035156
Outputs:
- sigma: float32 [9600, 600], P('chol', 'virt')
All inputs are finite; a program needn't handle non-finite values.
Results may differ from a plain program's by a relative error of at most 0.0042.
Values may be sent and summed in bfloat16 or wider, within the bound.
A program may use at most 128 MiB of HBM per device.

v0:
```python
import jax
import jax.numpy as jnp
from jax import lax
from jax.sharding import PartitionSpec as P


def joined_along(tiles, dim):
    tiles = jnp.moveaxis(tiles, 0, dim)
    lengths = tiles.shape
    return tiles.reshape(*lengths[:dim], lengths[dim] * lengths[dim + 1], *lengths[dim + 2 :])


def piecewise(x, axis, dim, work, out_dim):
    span = x.shape[dim]
    pieces = jnp.split(x, 2, axis=dim) if span % 2 == 0 else [x]
    leading = jnp.arange(lax.axis_size(axis)) * span
    tiles = [lax.all_gather(slab, axis) for slab in pieces]
    made = [jax.vmap(work)(b, leading + k * (span // len(pieces))) for k, b in enumerate(tiles)]
    return joined_along(jnp.concatenate(made, axis=out_dim + 1), out_dim)


def in_blocks(x, dim, length):
    lengths = x.shape
    tiles = x.reshape(*lengths[:dim], length, lengths[dim] // length, *lengths[dim + 1 :])
    return jnp.moveaxis(tiles, dim, 0)


def sum_at_owner(x, axis, dim):
    tiles = in_blocks(x, dim, lax.axis_size(axis))
    arrived = lax.all_to_all(tiles, axis, split_axis=0, concat_axis=0, tiled=True)
    return arrived.astype(jnp.float32).sum(axis=0)


def shards(amplitudes, chol_vectors):
    vec_count, row_share, orbitals = chol_vectors.shape
    turned = jnp.transpose(chol_vectors, (1, 2, 0)).reshape(row_share, orbitals * vec_count)
    local_flat = chol_vectors.reshape(vec_count * row_share, orbitals)
    ladder_half = jnp.dot(
        lax.all_gather(amplitudes, "chol", axis=0, tiled=True),
        local_flat.T,
        preferred_element_type=jnp.float32,
    ).astype(jnp.bfloat16)
    combos = ladder_half.shape[0] // orbitals
    half_blocks = ladder_half.reshape(combos, orbitals * vec_count, row_share)

    def contract(segment, offset):
        return jnp.einsum("ak,nkb->nab", segment, half_blocks, preferred_element_type=jnp.float32)

    sigma_terms = piecewise(turned, "virt", 0, contract, 1)
    sigma_terms = sigma_terms.reshape(combos * orbitals, row_share)
    return sum_at_owner(sigma_terms.astype(jnp.bfloat16), "chol", 0)


def solution(mesh):
    placed = (P("chol", None), P("chol", "virt", None))
    return jax.shard_map(
        shards, mesh=mesh, in_specs=placed, out_specs=P("chol", "virt"), check_vma=False
    )
```

profile of v0, /device:TPU:64, one launch (start us, length us, event | category | flops | bytes accessed | tf_op | source)
XLA Modules:
  0.0 389.9 jit_solution(3261966386860908832)
XLA Ops:
  6.5 0.0 all-gather.6.cloned.1.call-start
  6.5 0.7 all-gather.6.cloned.1.call-update
  7.3 0.0 all-gather.4.cloned.1.call-start
  7.3 2.6 copy.12
  9.9 2.0 copy.13
  11.9 0.0 all-gather.4.cloned.1.call-update
  12.0 1.2 copy.10
  13.2 0.4 reshape.9
  13.6 193.8 %all-gather.6.cloned.1.call-done = bf16[32,300,600]{2,1,0:T(8,128)(2,1)} async-done(((bf16[1,300,600]{2,1,0:T(8,128)(2,1)}), bf16[32,300,600]{2,1,0:T(8,128)(2,1)}) %all-gather.6.cloned.1.call-update) | async-done | bytes 11520016 | tf_op jit(solution)/shard_map/all_gather | solution.py:39
  207.4 16.6 %reshape.12 = bf16[9600,600]{1,0:T(8,128)(2,1)} reshape(bf16[32,300,600]{2,1,0:T(8,128)(2,1)} %all-gather.6.cloned.1.call-done) | data formatting | bytes 23040000
  224.0 21.0 %convolution_convert_fusion = bf16[9600,600]{0,1:T(8,128)(2,1)} fusion(bf16[9600,600]{1,0:T(8,128)(2,1)} %reshape.12, bf16[600,600]{1,0:T(8,128)(2,1)S(1)} %reshape.9), kind=kOutput, calls=%fused_computation.2 | convolution fusion | flops 6917760000 | bytes 23760000 | tf_op jit(solution)/shard_map/dot_general | solution.py:38
  245.0 16.8 %copy.11 = bf16[9600,600]{1,0:T(8,128)(2,1)} copy(bf16[9600,600]{0,1:T(8,128)(2,1)} %convolution_convert_fusion) | data formatting | bytes 23040000 | tf_op jit(solution)/shard_map/convert_element_type | solution.py:42
  261.8 30.4 %reshape.10 = bf16[16,4800,75]{2,1,0:T(8,128)(2,1)} reshape(bf16[9600,600]{1,0:T(8,128)(2,1)} %copy.11) | data formatting | bytes 23040000 | tf_op jit(solution)/shard_map/reshape | solution.py:44
  292.2 0.0 all-gather.4.cloned.1.call-done
  292.2 26.0 %convert_bitcast_fusion = bf16[16,8,75,75]{2,3,1,0:T(8,128)(2,1)S(1)} fusion(bf16[8,75,4800]{2,1,0:T(8,128)(2,1)} %all-gather.4.cloned.1.call-done, bf16[16,4800,75]{2,1,0:T(8,128)(2,1)} %reshape.10), kind=kOutput, calls=%fused_computation.5 | convolution fusion | flops 6912719872 | bytes 18720000 | tf_op jit(solution)/shard_map/vmap(ak,nkb->nab)/dot_general | solution.py:47
  318.2 0.6 copy.15
  318.8 2.8 convert_element_type.19
  321.6 2.2 copy.16
  323.8 58.3 %all_to_all.5 = bf16[32,300,75]{1,2,0:T(8,128)(2,1)S(1)} all-to-all(bf16[32,300,75]{1,2,0:T(8,128)(2,1)S(1)} %copy.16), channel_id=1, replica_groups=mesh['chol'=32,'virt'=8] {'chol'}, dimensions={0} | all-to-all | bytes 2880000 | tf_op jit(solution)/shard_map/all_to_all | solution.py:30
  382.1 1.0 convert_reduce_fusion
Async XLA Ops:
  6.5 200.8 %all-gather.6.cloned.1.call-start = ((), (), s32[]{:S(2)}) async-start(), calls=%async_computation.2 | async-start | bytes 12840960 | tf_op jit(solution)/shard_map/all_gather | solution.py:39
  7.3 284.9 %all-gather.4.cloned.1.call-start = ((), (), s32[]{:S(2)}) async-start(), calls=%async_computation.1 | async-start | bytes 7004160 | tf_op jit(solution)/shard_map/all_gather | solution.py:17
Sparse Core Ops, SparseCore 0:
  10.7 196.5 all-gather.5
  209.2 68.6 all-gather.3
where the time goes:
time: 392 us; the launch traced here: 390 us
  waiting for transfers between devices  195 us (50%)
  local copies, waits for them, and re-layouts  75.6 us (19%)
  blocking collectives  58.3 us (15%)
  matrix products  46.9 us (12%)
  between operations  13.4 us (3%)
    all_gather x1, waiting for transfers between devices, shards(): lax.all_gather(amplitudes, 'chol', axis=0, tiled=True)  194 us
    all_to_all x1, blocking collectives, sum_at_owner(): lax.all_to_all(tiles, axis, split_axis=0, concat_axis=0, tiled=True)  58.3 us
    reshape x1, local copies, waits for them, and re-layouts, shards(): half_blocks = ladder_half.reshape(combos, orbitals * vec_count, row_share)  30.4 us
    dot_general x1, matrix products, contract(): jnp.einsum('ak,nkb->nab', segment, half_blocks, preferred_element_type=jn...  26 us
    dot_general x1, matrix products, shards(): jnp.dot(lax.all_gather(amplitudes, 'chol', axis=0, tiled=True), local_fla...  21 us
    unnamed x2, local copies, waits for them, and re-layouts  17.9 us
    convert_element_type x1, local copies, waits for them, and re-layouts, shards(): ladder_half = jnp.dot(lax.all_gather(amplitudes, 'chol', axis=0, tiled=Tr...  16.8 us
  transfers between devices with their start and end apart: 2, of which 1 were waited for; matrix products, arithmetic and copies ran while one was open for 23% of the time, Pallas kernels for 0%

commit v1 on v0

v1 whole, which is shorter than its diff:
```python
import jax
import jax.numpy as jnp
from jax import lax
from jax.experimental import pallas as pl
from jax.experimental.pallas import tpu as pltpu
from jax.sharding import PartitionSpec as P

BF, F32 = jnp.bfloat16, jnp.float32
MESH = pl.DeviceIdType.MESH
NT = (((1,), (1,)), ((), ()))
V, W = 600, 640
TB, TW = 300, 304
LB, LW = 75, 80
SW = 320
N_SEND = 160


def kernel(t_in, l_in, out, lr, rb, lk, tb, tn, h, acc, sb,
           rxb1, rxb2, rya1, rya2, ryb1, ryb2, rxa1, rxa2, fin, zs, zr,
           send_sem, l_sem, rb_sem, t_sem, rxb_sem, rya_sem, ryb_sem, rxa_sem, z_sem):
    ci, vj = lax.axis_index("chol"), lax.axis_index("virt")
    zh, y, x = ci // 16, (ci // 4) % 4, ci % 4
    zl, core = vj // 2, vj % 2
    xp, xf, xm = (x + 1) % 4, (x + 2) % 4, (x + 3) % 4
    yp, ym = (y + 1) % 4, (y + 3) % 4
    end = jnp.logical_or(zl == 0, zl == 3)
    mid = jnp.logical_not(end)
    cls = y % 2 == core
    non = jnp.logical_not(cls)
    nh = jnp.where(end, 1 - zh, zh)
    ph = zl // 2
    d2 = jnp.where(zl < 2, 2, -2)
    yi, ip, im = y // 2, yp // 2, ym // 2

    def dev(chol, virt):
        return {"chol": chol, "virt": virt}

    def dev_x(v):
        return dev(zh * 16 + y * 4 + v, vj)

    def dev_y(v):
        return dev(zh * 16 + v * 4 + x, vj)

    partner = dev(ci, vj + 1 - 2 * core)

    barrier = pltpu.get_barrier_semaphore()
    spot = zh * 8 + vj
    for o in range(1, 16):
        other = (spot + o) % 16
        pl.semaphore_signal(barrier, inc=1, device_id=dev((other // 8) * 16 + y * 4 + x, other % 8), device_id_type=MESH)
    for there in (dev_x(xp), dev_x(xm), dev_y(yp), dev_y(ym)):
        pl.semaphore_signal(barrier, inc=1, device_id=there, device_id_type=MESH)
    pl.semaphore_wait(barrier, 19)

    pending = []

    def when(cond, work):
        if cond is None:
            work()
        else:
            pl.when(cond)(work)

    def send(cond, src, dst, sem, there):
        copy = pltpu.make_async_remote_copy(
            src_ref=src, dst_ref=dst, send_sem=send_sem.at[len(pending)], recv_sem=sem,
            device_id=there, device_id_type=MESH)
        pending.append((cond, copy))
        when(cond, copy.start)

    def arrived(cond, region, sem):
        when(cond, pltpu.make_async_copy(region, region, sem).wait)

    def own_l(half, pair):
        return l_in.at[pl.ds(half * 4 + pair * 2, 2)]

    def l_at(pair, j):
        return lr.at[pair, :, j]

    up, down = dev(ci, (vj + d2) % 8), dev(ci, (vj - d2 + 8) % 8)
    j1, j2, j3 = (vj + d2 + 8) % 8, (vj + 2 * d2 + 8) % 8, (vj + 3 * d2 + 8) % 8
    je = (vj - d2 + 8) % 8

    def l_first(pair):
        send(end, own_l(1 - ph, pair), rb.at[pair], rb_sem.at[pair], up)
        send(mid, own_l(1 - ph, pair), l_at(pair, vj), l_sem.at[pair, vj], up)
        send(mid, own_l(ph, pair), l_at(pair, vj), l_sem.at[pair, vj], down)
        send(end, own_l(ph, pair), l_at(pair, vj), l_sem.at[pair, vj], up)

    def l_own(pair):
        send(None, own_l(ph, pair), l_at(pair, vj), l_sem.at[pair, vj], partner)
        pltpu.make_async_copy(own_l(ph, pair), l_at(pair, vj), l_sem.at[pair, vj]).start()

    def l_arrived(cond, pair, j):
        arrived(cond, l_at(pair, j), l_sem.at[pair, j])

    def l_pass(cond, pair, j, there):
        send(cond, l_at(pair, j), l_at(pair, j), l_sem.at[pair, j], there)

    def l_relay_end(pair):
        arrived(mid, rb.at[pair], rb_sem.at[pair])
        send(mid, rb.at[pair], l_at(pair, je), l_sem.at[pair, je], up)

    def l_relay_across(pair, j):
        l_arrived(mid, pair, j)
        l_pass(mid, pair, j, down)
        l_pass(mid, pair, j, partner)

    def l_share(cond, pair, j):
        l_arrived(cond, pair, j)
        l_pass(cond, pair, j, partner)

    A, A0, A1 = pl.ds(0, 160), pl.ds(0, 80), pl.ds(80, 80)
    B, B0, B1 = pl.ds(160, 144), pl.ds(160, 80), pl.ds(240, 64)

    def t_send(cond, i, xs, rows, kind, there):
        send(cond, tb.at[i, xs, rows], tb.at[i, xs, rows], t_sem.at[i, xs, kind], there)

    def t_arrived(cond, i, xs, rows, kind):
        arrived(cond, tb.at[i, xs, rows], t_sem.at[i, xs, kind])

    border = dev((1 - zh) * 16 + y * 4 + x, (3 - zl) * 2 + core)
    end_cls, mid_cls = jnp.logical_and(end, cls), jnp.logical_and(mid, cls)
    for rows, kind in ((B, 2), (A, 0)):
        send(end_cls, t_in.at[rows], tb.at[yi, x, rows], t_sem.at[yi, x, kind], border)
        when(mid_cls, pltpu.make_async_copy(t_in.at[rows], tb.at[yi, x, rows], t_sem.at[yi, x, kind]).start)
    l_first(0)
    l_first(1)
    t_arrived(cls, yi, x, B, 2)
    t_arrived(cls, yi, x, A, 0)
    for v in (xp, xm):
        t_send(cls, yi, x, A, 0, dev_x(v))
    for v in (yp, ym):
        t_send(cls, yi, x, B, 2, dev_y(v))
    for v in (xp, xm):
        t_send(cls, yi, x, B, 2, dev_x(v))
    for v in (yp, ym):
        t_send(cls, yi, x, A, 0, dev_y(v))
    l_own(0)
    l_own(1)
    tn[:, V:, :] = jnp.zeros((4, W - V, W), BF)

    t_arrived(non, im, x, B, 2)
    t_arrived(non, ip, x, B, 2)
    t_send(non, im, x, B0, 2, dev_y(yp))
    t_send(non, ip, x, B1, 3, dev_y(ym))
    for i in (im, ip):
        for v in (xp, xm):
            t_send(non, i, x, B, 2, dev_x(v))
    t_arrived(cls, yi, xm, A, 0)
    t_arrived(cls, yi, xp, A, 0)
    t_send(cls, yi, xm, A0, 0, dev_x(xp))
    t_send(cls, yi, xp, A1, 1, dev_x(xm))
    for xs in (xm, xp):
        for v in (yp, ym):
            t_send(cls, yi, xs, A, 0, dev_y(v))
    l_relay_end(0)
    l_relay_across(0, j1)
    l_share(end, 0, j1)
    t_arrived(cls, 1 - yi, x, B0, 2)
    t_arrived(cls, 1 - yi, x, B1, 3)
    for v in (xp, xm):
        t_send(cls, 1 - yi, x, B, 2, dev_x(v))
    t_arrived(cls, yi, xf, A0, 0)
    t_arrived(cls, yi, xf, A1, 1)
    for v in (yp, ym):
        t_send(cls, yi, xf, A, 0, dev_y(v))

    def a4(xs):
        t_arrived(non, im, xs, A, 0)
        t_arrived(non, ip, xs, A, 0)
        t_send(non, im, xs, A0, 0, dev_y(yp))
        t_send(non, ip, xs, A1, 1, dev_y(ym))

    def b4(i):
        t_arrived(None, i, xm, B, 2)
        t_arrived(None, i, xp, B, 2)
        t_send(None, i, xm, B0, 2, dev_x(xp))
        t_send(None, i, xp, B1, 3, dev_x(xm))

    a4(x)
    b4(yi)
    l_share(mid, 0, je)
    l_relay_across(1, j1)
    l_share(end, 1, j1)
    a4(xm)
    a4(xp)
    b4(1 - yi)
    l_relay_across(0, j2)
    l_relay_end(1)
    a4(xf)
    l_share(end, 0, j2)
    for i in (0, 1):
        t_arrived(None, i, xf, B0, 2)
        t_arrived(None, i, xf, B1, 3)
    for xs in range(4):
        t_arrived(cls, 1 - yi, xs, A0, 0)
        t_arrived(cls, 1 - yi, xs, A1, 1)
    l_share(mid, 1, je)
    l_relay_across(1, j2)
    l_share(end, 0, j3)

    for n in range(4):
        i, k = n // 2, 2 * (n % 2)
        tn[n, 0:TB, :] = tb[i, k, 0:TB, :]
        tn[n, TB:V, :] = tb[i, k + 1, 0:TB, :]

    l_own_j = [2 * s + 1 - core for s in range(4)]
    for pair in (0,):
        l_arrived(None, pair, vj)
        for j in l_own_j:
            l_arrived(None, pair, j)

    def lay(pair):
        both = lr[pair].reshape(2, W, W)
        lk[:, :W] = both[0]
        lk[:, W:] = both[1]

    def halves(pair, n0, n1):
        for k, n in enumerate((n0, n1)):
            half = lax.dot_general(tn[n], lr[pair].reshape(2 * W, W), NT, preferred_element_type=F32).astype(BF)
            h[:W, k * W:(k + 1) * W] = half[:, :W]
            h[W:, k * W:(k + 1) * W] = half[:, W:]
        return jnp.dot(lk[...], h[...], preferred_element_type=F32)

    lay(0)

    def first(g, carry):
        acc[g] = halves(0, 2 * g, 2 * g + 1)
        return carry

    lax.fori_loop(0, 2, first, 0)
    l_share(end, 1, j2)
    l_share(end, 1, j3)
    l_arrived(None, 1, vj)
    for j in l_own_j:
        l_arrived(None, 1, j)
    lay(1)

    def second(g, carry):
        total = acc[g] + halves(1, 2 * g, 2 * g + 1)
        for k in range(2):
            block = total[:, k * W:(k + 1) * W].astype(BF)
            sb[g, 2 * k] = block[:SW]
            sb[g, 2 * k + 1] = block[SW:]
        return carry

    lax.fori_loop(0, 2, second, 0)

    A, A0, A1 = pl.ds(0, 160), pl.ds(0, 80), pl.ds(80, 80)
    B, B0, B1 = pl.ds(160, 160), pl.ds(160, 80), pl.ds(240, 80)

    def add(i, xs, rows, *others):
        total = sb[i, xs, rows, :].astype(F32)
        for other in others:
            total = total + other[...].astype(F32)
        return total

    def put(cond, i, xs, rows, *others):
        def work():
            sb[i, xs, rows, :] = add(i, xs, rows, *others).astype(BF)
        when(cond, work)

    for i in (0, 1):
        send(None, sb.at[i, xf, B0], rxb1.at[0, i], rxb_sem.at[0, 0, i], dev_x(xp))
        send(None, sb.at[i, xf, B1], rxb1.at[1, i], rxb_sem.at[0, 1, i], dev_x(xm))
    for xs in range(4):
        send(cls, sb.at[1 - yi, xs, A0], rya1.at[0, xs], rya_sem.at[0, 0, xs], dev_y(yp))
        send(cls, sb.at[1 - yi, xs, A1], rya1.at[1, xs], rya_sem.at[0, 1, xs], dev_y(ym))
    for i in (0, 1):
        arrived(None, rxb1.at[0, i], rxb_sem.at[0, 0, i])
        put(None, i, xp, B0, rxb1.at[0, i])
        send(None, sb.at[i, xp, B], rxb2.at[0, i], rxb_sem.at[1, 0, i], dev_x(xp))
        arrived(None, rxb1.at[1, i], rxb_sem.at[0, 1, i])
        put(None, i, xm, B1, rxb1.at[1, i])
        send(None, sb.at[i, xm, B], rxb2.at[1, i], rxb_sem.at[1, 1, i], dev_x(xm))
    for xs in range(4):
        arrived(non, rya1.at[0, xs], rya_sem.at[0, 0, xs])
        put(non, ip, xs, A0, rya1.at[0, xs])
        send(non, sb.at[ip, xs, A], rya2.at[0, xs], rya_sem.at[1, 0, xs], dev_y(yp))
        arrived(non, rya1.at[1, xs], rya_sem.at[0, 1, xs])
        put(non, im, xs, A1, rya1.at[1, xs])
        send(non, sb.at[im, xs, A], rya2.at[1, xs], rya_sem.at[1, 1, xs], dev_y(ym))
    for i in (0, 1):
        arrived(None, rxb2.at[0, i], rxb_sem.at[1, 0, i])
        arrived(None, rxb2.at[1, i], rxb_sem.at[1, 1, i])
        put(None, i, x, B, rxb2.at[0, i], rxb2.at[1, i])
    send(cls, sb.at[1 - yi, x, B0], ryb1.at[0], ryb_sem.at[0, 0], dev_y(yp))
    send(cls, sb.at[1 - yi, x, B1], ryb1.at[1], ryb_sem.at[0, 1], dev_y(ym))
    for xs in range(4):
        arrived(cls, rya2.at[0, xs], rya_sem.at[1, 0, xs])
        arrived(cls, rya2.at[1, xs], rya_sem.at[1, 1, xs])
        put(cls, yi, xs, A, rya2.at[0, xs], rya2.at[1, xs])
    send(cls, sb.at[yi, xf, A0], rxa1.at[0], rxa_sem.at[0, 0], dev_x(xp))
    send(cls, sb.at[yi, xf, A1], rxa1.at[1], rxa_sem.at[0, 1], dev_x(xm))
    arrived(non, ryb1.at[0], ryb_sem.at[0, 0])
    put(non, ip, x, B0, ryb1.at[0])
    send(non, sb.at[ip, x, B], ryb2.at[0], ryb_sem.at[1, 0], dev_y(yp))
    arrived(non, ryb1.at[1], ryb_sem.at[0, 1])
    put(non, im, x, B1, ryb1.at[1])
    send(non, sb.at[im, x, B], ryb2.at[1], ryb_sem.at[1, 1], dev_y(ym))
    arrived(cls, rxa1.at[0], rxa_sem.at[0, 0])
    put(cls, yi, xp, A0, rxa1.at[0])
    send(cls, sb.at[yi, xp, A], rxa2.at[0], rxa_sem.at[1, 0], dev_x(xp))
    arrived(cls, rxa1.at[1], rxa_sem.at[0, 1])
    put(cls, yi, xm, A1, rxa1.at[1])
    send(cls, sb.at[yi, xm, A], rxa2.at[1], rxa_sem.at[1, 1], dev_x(xm))
    for k in range(2):
        arrived(cls, ryb2.at[k], ryb_sem.at[1, k])
        arrived(cls, rxa2.at[k], rxa_sem.at[1, k])

    @pl.when(cls)
    def _():
        fin[0:160, :] = add(yi, x, A, rxa2.at[0], rxa2.at[1])
        fin[160:320, :] = add(yi, x, B, ryb2.at[0], ryb2.at[1])
        fin[320:, :] = jnp.zeros((64, W), F32)
        zs[...] = fin[...].T.astype(BF).reshape(8, LW, 384)

    for o in (1, 2, 3, 4, 5, 6, 7):
        j = (vj + o) % 8
        send(cls, zs.at[j], zr.at[zl], z_sem.at[zl], dev(nh * 16 + y * 4 + x, j))
    send(end_cls, zs.at[vj], zr.at[zl], z_sem.at[zl], dev(nh * 16 + y * 4 + x, vj))
    when(mid_cls, pltpu.make_async_copy(zs.at[vj], zr.at[zl], z_sem.at[zl]).start)
    for s in range(4):
        arrived(None, zr.at[s], z_sem.at[s])
    total = zr[0].astype(F32) + zr[1].astype(F32) + zr[2].astype(F32) + zr[3].astype(F32)
    fin[0:LW, 0:384] = total
    turned = fin[0:128, 0:384].T
    for q in range(4):
        out[q * LB:(q + 1) * LB, :] = turned[q * LW:q * LW + LB, :LB]

    for cond, copy in pending:
        when(cond, copy.wait_send)


def shards(amplitudes, chol_vectors):
    t_in = jnp.pad(amplitudes, ((0, TW - TB), (0, W - V)))
    l_in = jnp.pad(chol_vectors, ((0, 0), (0, LW - LB), (0, W - V)))
    dma = pltpu.SemaphoreType.DMA
    vmem = pltpu.VMEM
    return pl.pallas_call(
        kernel,
        out_shape=jax.ShapeDtypeStruct((TB, LB), F32),
        in_specs=[pl.BlockSpec(memory_space=pltpu.VMEM)] * 2,
        out_specs=pl.BlockSpec(memory_space=pltpu.VMEM),
        scratch_shapes=[
            vmem((2, 2, 8, LW, W), BF), vmem((2, 2, LW, W), BF), vmem((W, 2 * W), BF),
            vmem((2, 4, TW, W), BF), vmem((4, W, W), BF), vmem((2 * W, 2 * W), BF),
            vmem((2, W, 2 * W), F32), vmem((2, 4, SW, W), BF),
            vmem((2, 2, 80, W), BF), vmem((2, 2, 160, W), BF),
            vmem((2, 4, 80, W), BF), vmem((2, 4, 160, W), BF),
            vmem((2, 80, W), BF), vmem((2, 160, W), BF), vmem((2, 80, W), BF), vmem((2, 160, W), BF),
            vmem((384, W), F32), vmem((8, LW, 384), BF), vmem((4, LW, 384), BF),
            dma((N_SEND,)), dma((2, 8)), dma((2,)), dma((2, 4, 4)),
            dma((2, 2, 2)), dma((2, 2, 4)), dma((2, 2)), dma((2, 2)), dma((4,)),
        ],
        compiler_params=pltpu.CompilerParams(
            collective_id=0, has_side_effects=True, vmem_limit_bytes=60 << 20),
        name="ladder",
    )(t_in, l_in)


def solution(mesh):
    placed = (P("chol", None), P("chol", "virt", None))
    return jax.shard_map(
        shards, mesh=mesh, in_specs=placed, out_specs=P("chol", "virt"), check_vma=False
    )
```

time: 392 us -> 103 us (0.26)
  the two profiles are of different devices: /device:TPU:64 before, /device:TPU:67 now
where the time goes in v1:
time: 103 us
  Pallas kernels  98.5 us (96%)
  local copies, waits for them, and re-layouts  4.69 us (5%)
    pallas_call x1, Pallas kernels, shards(): pl.pallas_call(kernel, out_shape=jax.ShapeDtypeStruct((TB, LB), F32), in_...  98.5 us

profile of v1, /device:TPU:67, one launch (start us, length us, event | category | flops | bytes accessed | tf_op | source)
XLA Modules:
  0.0 103.2 jit_solution(15290890182697867225)
XLA Ops:
  0.0 1.2 %copy.3 = bf16[8,75,600]{2,1,0:T(8,128)(2,1)S(1)} copy(bf16[8,75,600]{2,0,1:T(8,128)(2,1)} %param.3) | data formatting | bytes 1440000 | tf_op args[1]
  1.2 0.0 copy-start
  1.2 1.0 pad.9.l_in
  2.2 0.0 copy-done
  2.2 0.8 pad.8.t_in
  3.0 98.5 %ladder.1 = f32[300,75]{1,0:T(8,128)} custom-call(bf16[304,640]{1,0:T(8,128)(2,1)} %pad.8.t_in, bf16[8,80,640]{2,1,0:T(8,128)(2,1)} %pad.9.l_in), custom_call_target="tpu_custom_call" | custom-call | tf_op jit(solution)/shard_map/ladder/pallas_call | solution.py:340
  101.5 1.7 %copy.4 = f32[300,75]{0,1:T(8,128)} copy(f32[300,75]{1,0:T(8,128)} %ladder.1) | data formatting | bytes 180000 | tf_op jit(solution)/shard_map/ladder/pallas_call | solution.py:340
Async XLA Ops:
  1.2 1.0 copy-start

commit v2 on v1

v2 whole, which is shorter than its diff:
```python
import jax
import jax.numpy as jnp
from jax import lax
from jax.experimental import pallas as pl
from jax.experimental.pallas import tpu as pltpu
from jax.sharding import PartitionSpec as P

BF, F32 = jnp.bfloat16, jnp.float32
MESH = pl.DeviceIdType.MESH
NT = (((1,), (1,)), ((), ()))
V, W = 600, 640
TB, TW = 300, 304
LB, LW = 75, 80
SW = 320
N_SEND = 110


def kernel(t_raw, l_raw, out, t_in, l_in, lr, rb, lk, tb, tn, h, acc, sb,
           rxb1, rxb2, rya1, rya2, ryb1, ryb2, rxa1, rxa2, fin, zs, zr,
           send_sem, l_sem, rb_sem, t_sem, rxb_sem, rya_sem, ryb_sem, rxa_sem, z_sem, line_sem):
    ci, vj = lax.axis_index("chol"), lax.axis_index("virt")
    zh, y, x = ci // 16, (ci // 4) % 4, ci % 4
    zl, core = vj // 2, vj % 2
    xp, xf, xm = (x + 1) % 4, (x + 2) % 4, (x + 3) % 4
    yp, ym = (y + 1) % 4, (y + 3) % 4
    end = jnp.logical_or(zl == 0, zl == 3)
    mid = jnp.logical_not(end)
    cls = y % 2 == core
    non = jnp.logical_not(cls)
    nh = jnp.where(end, 1 - zh, zh)
    ph = zl // 2
    d2 = jnp.where(zl < 2, 2, -2)
    yi, ip, im = y // 2, yp // 2, ym // 2
    yf = (y + 2) % 4

    def row_of(g, xs):
        return (xs // 2 + g) % 2

    def cols_of(g, i):
        first_col = 2 * ((i + g) % 2)
        return first_col, first_col + 1

    def both(a, b):
        return jnp.logical_and(a, b)

    g_own = (x // 2 + yi) % 2
    g_near = jnp.where(end, 1, 0)
    g_far = 1 - g_near
    z_owner = (nh + g_own) % 2

    def dev(chol, virt):
        return {"chol": chol, "virt": virt}

    def dev_x(v):
        return dev(zh * 16 + y * 4 + v, vj)

    def dev_y(v):
        return dev(zh * 16 + v * 4 + x, vj)

    partner = dev(ci, vj + 1 - 2 * core)

    border = dev((1 - zh) * 16 + y * 4 + x, (3 - zl) * 2 + core)
    behind = dev((1 - zh) * 16 + y * 4 + x, (3 - zl) * 2 + core - d2)
    ahead = dev((1 - zh) * 16 + y * 4 + x, (3 - zl + d2 // 2) * 2 + core)
    up, down = dev(ci, (vj + d2) % 8), dev(ci, (vj - d2 + 8) % 8)

    barrier = pltpu.get_barrier_semaphore()
    for there in (dev_x(xp), dev_x(xm), dev_x(xf), dev_y(yp), dev_y(ym), dev_y(yf), up, partner):
        pl.semaphore_signal(barrier, inc=1, device_id=there, device_id_type=MESH)

    @pl.when(end)
    def _():
        pl.semaphore_signal(barrier, inc=1, device_id=border, device_id_type=MESH)
        pl.semaphore_signal(barrier, inc=1, device_id=behind, device_id_type=MESH)

    @pl.when(mid)
    def _():
        pl.semaphore_signal(barrier, inc=1, device_id=down, device_id_type=MESH)
        pl.semaphore_signal(barrier, inc=1, device_id=ahead, device_id_type=MESH)

    t_in[...] = jnp.zeros_like(t_in)
    t_in[:TB, :V] = t_raw[...]
    l_in[:, LB - 3:, :] = jnp.zeros((8, LW - LB + 3, W), BF)
    l_in[:, :, V - 88:] = jnp.zeros((8, LW, W - V + 88), BF)
    l_in[:, :LB, :V] = l_raw[...]
    tn[:, V:, :] = jnp.zeros((4, W - V, W), BF)
    pl.semaphore_wait(barrier, 10)

    pending = []

    def when(cond, work):
        if cond is None:
            work()
        else:
            pl.when(cond)(work)

    def send(cond, src, dst, sem, there):
        copy = pltpu.make_async_remote_copy(
            src_ref=src, dst_ref=dst, send_sem=send_sem.at[len(pending)], recv_sem=sem,
            device_id=there, device_id_type=MESH)
        pending.append((cond, copy.wait_send))
        when(cond, copy.start)

    def arrived(cond, region, sem):
        when(cond, pltpu.make_async_copy(region, region, sem).wait)

    def own_l(half, pair):
        return l_in.at[pl.ds(half * 4 + pair * 2, 2)]

    def l_at(pair, j):
        return lr.at[pair, :, j]

    j1, j2, j3 = (vj + d2 + 8) % 8, (vj + 2 * d2 + 8) % 8, (vj + 3 * d2 + 8) % 8
    je = (vj - d2 + 8) % 8

    def l_first(pair):
        send(end, own_l(1 - ph, pair), rb.at[pair], rb_sem.at[pair], up)
        send(mid, own_l(1 - ph, pair), l_at(pair, vj), l_sem.at[pair, vj], up)
        send(mid, own_l(ph, pair), l_at(pair, vj), l_sem.at[pair, vj], down)
        send(end, own_l(ph, pair), l_at(pair, vj), l_sem.at[pair, vj], up)

    def l_own(pair):
        send(None, own_l(ph, pair), l_at(pair, vj), l_sem.at[pair, vj], partner)
        pltpu.make_async_copy(own_l(ph, pair), l_at(pair, vj), l_sem.at[pair, vj]).start()

    def l_arrived(cond, pair, j):
        arrived(cond, l_at(pair, j), l_sem.at[pair, j])

    def l_pass(cond, pair, j, there):
        send(cond, l_at(pair, j), l_at(pair, j), l_sem.at[pair, j], there)

    def l_relay_end(pair):
        arrived(mid, rb.at[pair], rb_sem.at[pair])
        send(mid, rb.at[pair], l_at(pair, je), l_sem.at[pair, je], up)

    def l_relay_across(pair, j):
        l_arrived(mid, pair, j)
        l_pass(mid, pair, j, down)
        l_pass(mid, pair, j, partner)

    def l_share(cond, pair, j):
        l_arrived(cond, pair, j)
        l_pass(cond, pair, j, partner)

    A, B = pl.ds(0, 160), pl.ds(160, 144)
    own_near, own_far = both(cls, g_own == g_near), both(cls, g_own == g_far)

    def t_at(i, xs, rows):
        return tb.at[i, xs, rows], t_sem.at[i, xs, 0 if rows is A else 1]

    def t_send(cond, i, xs, rows, theres):
        region, sem = t_at(i, xs, rows)
        copies = [pltpu.make_async_remote_copy(
            src_ref=region, dst_ref=region, send_sem=send_sem.at[len(pending)], recv_sem=sem,
            device_id=there, device_id_type=MESH) for there in theres]

        def work():
            for copy in copies:
                copy.start()

        when(cond, work)
        three = tb.at[0, pl.ds(0, 3), rows]
        pending.append((cond, pltpu.make_async_copy(three, three, send_sem.at[len(pending)]).wait))

    def t_arrived(cond, i, xs, rows):
        arrived(cond, *t_at(i, xs, rows))

    x_others, y_others = [dev_x(v) for v in (xp, xm, xf)], [dev_y(v) for v in (yp, ym, yf)]
    end_cls = both(end, cls)

    def t_start():
        for rows in (A, B):
            region, sem = t_at(yi, x, rows)
            send(both(end_cls, g_own == 0), t_in.at[rows], region, sem, border)
            send(both(end_cls, g_own == 1), t_in.at[rows], region, sem, behind)
            when(own_near, pltpu.make_async_copy(t_in.at[rows], region, sem).start)

    def t_own(cond):
        t_arrived(cond, yi, x, A)
        t_send(cond, yi, x, A, x_others)
        t_arrived(cond, yi, x, B)
        t_send(cond, yi, x, B, y_others)
        t_send(cond, yi, x, B, x_others)
        t_send(cond, yi, x, A, y_others)

    def t_second(g):
        for xs in cols_of(g, yi):
            t_arrived(both(cls, xs != x), yi, xs, A)
            t_send(both(cls, xs != x), yi, xs, A, y_others)
        i = row_of(g, x)
        cond = jnp.logical_or(non, i != yi)
        t_arrived(cond, i, x, B)
        t_send(cond, i, x, B, x_others)

    def t_join(g):
        for i in (0, 1):
            for xs in cols_of(g, i):
                t_arrived(jnp.logical_or(non, yi != i), i, xs, A)
                t_arrived(xs != x, i, xs, B)
            n, k = (g, 2 * g) if i == 0 else (3 - g, 2 * (1 - g))
            tn[n, 0:TB, :] = tb[i, k, 0:TB, :]
            tn[n, TB:V, :] = tb[i, k + 1, 0:TB, :]

    t_start()
    l_first(0)
    l_first(1)
    t_own(own_near)
    l_own(0)
    l_own(1)
    l_relay_end(0)
    l_relay_across(0, j1)
    l_share(end, 0, j1)
    t_own(own_far)
    t_second(g_near)
    l_share(mid, 0, je)
    l_relay_across(1, j1)
    l_share(end, 1, j1)
    l_relay_across(0, j2)
    l_relay_end(1)
    t_second(g_far)
    l_share(end, 0, j2)
    l_share(mid, 1, je)
    l_relay_across(1, j2)
    l_share(end, 0, j3)
    t_join(g_near)
    partner_j = [2 * s + 1 - core for s in range(4)]
    l_arrived(None, 0, vj)
    for j in partner_j:
        l_arrived(None, 0, j)

    def lay(pair):
        both = lr[pair].reshape(2, W, W)
        lk[:, :W] = both[0]
        lk[:, W:] = both[1]

    def first_half(pair, k, n):
        half = lax.dot_general(tn[n], lr[pair].reshape(2 * W, W), NT, preferred_element_type=F32).astype(BF)
        h[:W, k * W:(k + 1) * W] = half[:, :W]
        h[W:, k * W:(k + 1) * W] = half[:, W:]

    def join_halves(pair, g):
        first_half(pair, 0, g)
        first_half(pair, 1, 3 - g)

    lay(0)
    join_halves(0, g_near)
    acc[0] = jnp.dot(lk[...], h[...], preferred_element_type=F32)
    l_share(end, 1, j2)
    t_join(g_far)
    join_halves(0, g_far)
    acc[1] = jnp.dot(lk[...], h[...], preferred_element_type=F32)
    l_share(end, 1, j3)
    l_arrived(None, 1, vj)
    for j in partner_j:
        l_arrived(None, 1, j)

    @pl.when(end)
    def _():
        pl.semaphore_signal(line_sem, inc=1, device_id=border, device_id_type=MESH)

    lay(1)

    def second(order, g):
        total = acc[order] + jnp.dot(lk[...], h[...], preferred_element_type=F32)
        for k, c in ((0, g), (1, 1 - g)):
            block = total[:, k * W:(k + 1) * W].astype(BF)
            sb[k, 2 * c] = block[:SW]
            sb[k, 2 * c + 1] = block[SW:]

    A, A0, A1 = pl.ds(0, 160), pl.ds(0, 80), pl.ds(80, 80)
    B, B0, B1 = pl.ds(160, 160), pl.ds(160, 80), pl.ds(240, 80)

    def add(i, xs, rows, *others):
        total = sb[i, xs, rows, :].astype(F32)
        for other in others:
            total = total + other[...].astype(F32)
        return total

    def put(cond, i, xs, rows, *others):
        def work():
            sb[i, xs, rows, :] = add(i, xs, rows, *others).astype(BF)
        when(cond, work)

    def r1(g):
        i = row_of(g, xf)
        send(None, sb.at[i, xf, B0], rxb1.at[0, i], rxb_sem.at[0, 0, i], dev_x(xp))
        send(None, sb.at[i, xf, B1], rxb1.at[1, i], rxb_sem.at[0, 1, i], dev_x(xm))
        for xs in cols_of(g, 1 - yi):
            send(cls, sb.at[1 - yi, xs, A0], rya1.at[0, xs], rya_sem.at[0, 0, xs], dev_y(yp))
            send(cls, sb.at[1 - yi, xs, A1], rya1.at[1, xs], rya_sem.at[0, 1, xs], dev_y(ym))

    def r2(g):
        i = row_of(g, xp)
        arrived(None, rxb1.at[0, i], rxb_sem.at[0, 0, i])
        put(None, i, xp, B0, rxb1.at[0, i])
        send(None, sb.at[i, xp, B], rxb2.at[0, i], rxb_sem.at[1, 0, i], dev_x(xp))
        i = row_of(g, xm)
        arrived(None, rxb1.at[1, i], rxb_sem.at[0, 1, i])
        put(None, i, xm, B1, rxb1.at[1, i])
        send(None, sb.at[i, xm, B], rxb2.at[1, i], rxb_sem.at[1, 1, i], dev_x(xm))
        for k in range(2):
            xs = cols_of(g, ip)[k]
            arrived(non, rya1.at[0, xs], rya_sem.at[0, 0, xs])
            put(non, ip, xs, A0, rya1.at[0, xs])
            send(non, sb.at[ip, xs, A], rya2.at[0, xs], rya_sem.at[1, 0, xs], dev_y(yp))
            xs = cols_of(g, im)[k]
            arrived(non, rya1.at[1, xs], rya_sem.at[0, 1, xs])
            put(non, im, xs, A1, rya1.at[1, xs])
            send(non, sb.at[im, xs, A], rya2.at[1, xs], rya_sem.at[1, 1, xs], dev_y(ym))

    def r3(g):
        i = row_of(g, x)
        arrived(None, rxb2.at[0, i], rxb_sem.at[1, 0, i])
        arrived(None, rxb2.at[1, i], rxb_sem.at[1, 1, i])
        put(None, i, x, B, rxb2.at[0, i], rxb2.at[1, i])
        far = both(cls, i != yi)
        send(far, sb.at[1 - yi, x, B0], ryb1.at[0], ryb_sem.at[0, 0], dev_y(yp))
        send(far, sb.at[1 - yi, x, B1], ryb1.at[1], ryb_sem.at[0, 1], dev_y(ym))
        for xs in cols_of(g, yi):
            arrived(cls, rya2.at[0, xs], rya_sem.at[1, 0, xs])
            arrived(cls, rya2.at[1, xs], rya_sem.at[1, 1, xs])
            put(cls, yi, xs, A, rya2.at[0, xs], rya2.at[1, xs])
        far = both(cls, row_of(g, xf) == yi)
        send(far, sb.at[yi, xf, A0], rxa1.at[0], rxa_sem.at[0, 0], dev_x(xp))
        send(far, sb.at[yi, xf, A1], rxa1.at[1], rxa_sem.at[0, 1], dev_x(xm))

    def r4(g):
        i = row_of(g, x)
        to_up, to_down = both(non, i == ip), both(non, i == im)
        arrived(to_up, ryb1.at[0], ryb_sem.at[0, 0])
        put(to_up, ip, x, B0, ryb1.at[0])
        send(to_up, sb.at[ip, x, B], ryb2.at[0], ryb_sem.at[1, 0], dev_y(yp))
        arrived(to_down, ryb1.at[1], ryb_sem.at[0, 1])
        put(to_down, im, x, B1, ryb1.at[1])
        send(to_down, sb.at[im, x, B], ryb2.at[1], ryb_sem.at[1, 1], dev_y(ym))
        to_up, to_down = both(cls, row_of(g, xp) == yi), both(cls, row_of(g, xm) == yi)
        arrived(to_up, rxa1.at[0], rxa_sem.at[0, 0])
        put(to_up, yi, xp, A0, rxa1.at[0])
        send(to_up, sb.at[yi, xp, A], rxa2.at[0], rxa_sem.at[1, 0], dev_x(xp))
        arrived(to_down, rxa1.at[1], rxa_sem.at[0, 1])
        put(to_down, yi, xm, A1, rxa1.at[1])
        send(to_down, sb.at[yi, xm, A], rxa2.at[1], rxa_sem.at[1, 1], dev_x(xm))

    join_halves(1, g_near)
    second(0, g_near)
    r1(g_near)
    join_halves(1, g_far)
    r2(g_near)
    second(1, g_far)
    r1(g_far)
    r3(g_near)
    r2(g_far)
    pl.semaphore_wait(line_sem, 1)

    @pl.when(end)
    def _():
        pl.semaphore_signal(line_sem, inc=1, device_id=up, device_id_type=MESH)

    r4(g_near)
    r3(g_far)
    r4(g_far)
    for k in range(2):
        arrived(cls, ryb2.at[k], ryb_sem.at[1, k])
        arrived(cls, rxa2.at[k], rxa_sem.at[1, k])

    @pl.when(cls)
    def _():
        fin[0:160, :] = add(yi, x, A, rxa2.at[0], rxa2.at[1])
        fin[160:320, :] = add(yi, x, B, ryb2.at[0], ryb2.at[1])
        fin[320:, :] = jnp.zeros((64, W), F32)
        zs[...] = fin[...].T.astype(BF).reshape(8, LW, 384)

    away = z_owner != zh
    for o in range(8):
        j = (vj + o) % 8
        send(both(cls, away) if o == 0 else cls, zs.at[j], zr.at[zl], z_sem.at[zl], dev(z_owner * 16 + y * 4 + x, j))
    when(both(cls, z_owner == zh), pltpu.make_async_copy(zs.at[vj], zr.at[zl], z_sem.at[zl]).start)
    for s in range(4):
        arrived(None, zr.at[s], z_sem.at[s])
    total = zr[0].astype(F32) + zr[1].astype(F32) + zr[2].astype(F32) + zr[3].astype(F32)
    for q in range(4):
        out[:, q * LB:(q + 1) * LB] = total[:LB, q * LW:q * LW + LB]

    assert len(pending) <= N_SEND, len(pending)
    for cond, wait in pending:
        when(cond, wait)


def shards(amplitudes, chol_vectors):
    dma = pltpu.SemaphoreType.DMA
    vmem = pltpu.VMEM
    turned = pl.pallas_call(
        kernel,
        out_shape=jax.ShapeDtypeStruct((LB, TB), F32),
        in_specs=[pl.BlockSpec(memory_space=pltpu.VMEM)] * 2,
        out_specs=pl.BlockSpec(memory_space=pltpu.VMEM),
        scratch_shapes=[
            vmem((TW, W), BF), vmem((8, LW, W), BF),
            vmem((2, 2, 8, LW, W), BF), vmem((2, 2, LW, W), BF), vmem((W, 2 * W), BF),
            vmem((2, 4, TW, W), BF), vmem((4, W, W), BF), vmem((2 * W, 2 * W), BF),
            vmem((2, W, 2 * W), F32), vmem((2, 4, SW, W), BF),
            vmem((2, 2, 80, W), BF), vmem((2, 2, 160, W), BF),
            vmem((2, 4, 80, W), BF), vmem((2, 4, 160, W), BF),
            vmem((2, 80, W), BF), vmem((2, 160, W), BF), vmem((2, 80, W), BF), vmem((2, 160, W), BF),
            vmem((384, W), F32), vmem((8, LW, 384), BF), vmem((4, LW, 384), BF),
            dma((N_SEND,)), dma((2, 8)), dma((2,)), dma((2, 4, 2)),
            dma((2, 2, 2)), dma((2, 2, 4)), dma((2, 2)), dma((2, 2)), dma((4,)),
            pltpu.SemaphoreType.REGULAR,
        ],
        compiler_params=pltpu.CompilerParams(
            collective_id=0, has_side_effects=True, vmem_limit_bytes=52 << 20),
        name="ladder",
    )(amplitudes, chol_vectors)
    return turned.T


def solution(mesh):
    placed = (P("chol", None), P("chol", "virt", None))
    return jax.shard_map(
        shards, mesh=mesh, in_specs=placed, out_specs=P("chol", "virt"), check_vma=False
    )
```

time: 103 us -> 98.1 us (0.952)
  the two profiles are of different devices: /device:TPU:67 before, /device:TPU:7 now
where the time goes in v2:
time: 98.1 us; the launch traced here: 96.8 us
  Pallas kernels  94.9 us (97%)
  local copies, waits for them, and re-layouts  1.93 us (2%)
    pallas_call x1, Pallas kernels, shards(): pl.pallas_call(kernel, out_shape=jax.ShapeDtypeStruct((LB, TB), F32), in_...  94.9 us

profile of v2, /device:TPU:7, one launch (start us, length us, event | category | flops | bytes accessed | tf_op | source)
XLA Modules:
  0.0 96.8 jit_solution(9423399776919749388)
XLA Ops:
  0.0 0.0 copy-start
  0.0 1.3 %copy.3.l_raw = bf16[8,75,600]{2,1,0:T(8,128)(2,1)S(1)} copy(bf16[8,75,600]{2,0,1:T(8,128)(2,1)} %param.3) | data formatting | bytes 1440000 | tf_op args[1]
  1.3 0.0 copy-done
  1.3 94.9 %ladder.1 = f32[75,300]{1,0:T(8,128)S(1)} custom-call(bf16[300,600]{1,0:T(8,128)(2,1)S(1)} %copy-done, bf16[8,75,600]{2,1,0:T(8,128)(2,1)S(1)} %copy.3.l_raw), custom_call_target="tpu_custom_call" | custom-call | tf_op jit(solution)/shard_map/ladder/pallas_call | solution.py:392
  96.2 0.7 copy.5
Async XLA Ops:
  0.0 1.3 %copy-start = (bf16[300,600]{1,0:T(8,128)(2,1)S(1)}, bf16[300,600]{1,0:T(8,128)(2,1)}, u32[]{:S(2)}) copy-start(bf16[300,600]{1,0:T(8,128)(2,1)} %t_raw.1) | copy-start | bytes 1080004

commit v3 on v2

v3 whole, which is shorter than its diff:
```python
import jax
import jax.numpy as jnp
from jax import lax
from jax.experimental import pallas as pl
from jax.experimental.pallas import tpu as pltpu
from jax.sharding import PartitionSpec as P

BF, F32 = jnp.bfloat16, jnp.float32
MESH = pl.DeviceIdType.MESH
NT = (((1,), (1,)), ((), ()))
V, W = 600, 640
TB, TW = 300, 304
LB, LW = 75, 80
SW = 320
N_SEND = 84


def kernel(t_raw, l_raw, out, t_in, l_in, lr, lk, tb, tn, h, acc, sb,
           rxb, rya, ryb, rxa, fin, zs, zr,
           send_sem, l_sem, t_sem, rxb_sem, rya_sem, ryb_sem, rxa_sem, z_sem, line_sem):
    ci, vj = lax.axis_index("chol"), lax.axis_index("virt")
    zh, y, x = ci // 16, (ci // 4) % 4, ci % 4
    zl, core = vj // 2, vj % 2
    xp, xf, xm = (x + 1) % 4, (x + 2) % 4, (x + 3) % 4
    yp, ym = (y + 1) % 4, (y + 3) % 4
    end = jnp.logical_or(zl == 0, zl == 3)
    mid = jnp.logical_not(end)
    cls = y % 2 == core
    non = jnp.logical_not(cls)
    nh = jnp.where(end, 1 - zh, zh)
    ph = zl // 2
    d2 = jnp.where(zl < 2, 2, -2)
    yi, ip, im = y // 2, yp // 2, ym // 2
    yf = (y + 2) % 4

    def row_of(g, xs):
        return (xs // 2 + g) % 2

    def cols_of(g, i):
        first_col = 2 * ((i + g) % 2)
        return first_col, first_col + 1

    def both(a, b):
        return jnp.logical_and(a, b)

    g_own = (x // 2 + yi) % 2
    g_near = jnp.where(end, 1, 0)
    g_far = 1 - g_near
    z_owner = (nh + g_own) % 2

    def dev(chol, virt):
        return {"chol": chol, "virt": virt}

    def dev_x(v):
        return dev(zh * 16 + y * 4 + v, vj)

    def dev_y(v):
        return dev(zh * 16 + v * 4 + x, vj)

    partner = dev(ci, vj + 1 - 2 * core)

    border = dev((1 - zh) * 16 + y * 4 + x, (3 - zl) * 2 + core)
    behind = dev((1 - zh) * 16 + y * 4 + x, (3 - zl) * 2 + core - d2)
    ahead = dev((1 - zh) * 16 + y * 4 + x, (3 - zl + d2 // 2) * 2 + core)
    up, down = dev(ci, (vj + d2) % 8), dev(ci, (vj - d2 + 8) % 8)

    opposite = dev(ci, (vj + 2 * d2 + 8) % 8)

    barrier = pltpu.get_barrier_semaphore()
    for there in (dev_x(xp), dev_x(xm), dev_x(xf), dev_y(yp), dev_y(ym), dev_y(yf), up, opposite, partner):
        pl.semaphore_signal(barrier, inc=1, device_id=there, device_id_type=MESH)

    @pl.when(end)
    def _():
        pl.semaphore_signal(barrier, inc=1, device_id=border, device_id_type=MESH)
        pl.semaphore_signal(barrier, inc=1, device_id=behind, device_id_type=MESH)

    @pl.when(mid)
    def _():
        pl.semaphore_signal(barrier, inc=1, device_id=down, device_id_type=MESH)
        pl.semaphore_signal(barrier, inc=1, device_id=ahead, device_id_type=MESH)

    t_in[...] = jnp.zeros_like(t_in)
    t_in[:TB, :V] = t_raw[...]
    l_in[:, LB - 3:, :] = jnp.zeros((8, LW - LB + 3, W), BF)
    l_in[:, :, V - 88:] = jnp.zeros((8, LW, W - V + 88), BF)
    l_in[:, :LB, :V] = l_raw[...]
    tn[:, V:, :] = jnp.zeros((4, W - V, W), BF)
    pl.semaphore_wait(barrier, 11)

    pending = []

    def when(cond, work):
        if cond is None:
            work()
        else:
            pl.when(cond)(work)

    def send(cond, src, dst, sem, there):
        copy = pltpu.make_async_remote_copy(
            src_ref=src, dst_ref=dst, send_sem=send_sem.at[len(pending)], recv_sem=sem,
            device_id=there, device_id_type=MESH)
        pending.append((cond, copy.wait_send))
        when(cond, copy.start)

    def arrived(cond, region, sem):
        when(cond, pltpu.make_async_copy(region, region, sem).wait)

    def own_l(half, pair):
        return l_in.at[pl.ds(half * 4 + pair * 2, 2)]

    def l_at(pair, j):
        return lr.at[pair, :, j]

    j1, j2, j3 = (vj + d2 + 8) % 8, (vj + 2 * d2 + 8) % 8, (vj + 3 * d2 + 8) % 8
    je = (vj - d2 + 8) % 8

    def l_first():
        send(mid, own_l(1 - ph, 0), l_at(0, vj), l_sem.at[0, vj], up)
        for pair in (0, 1):
            send(mid, own_l(ph, pair), l_at(pair, vj), l_sem.at[pair, vj], down)
            send(end, own_l(ph, pair), l_at(pair, vj), l_sem.at[pair, vj], up)
            send(end, own_l(1 - ph, pair), l_at(pair, vj), l_sem.at[pair, vj], opposite)

    def l_own(pair):
        send(None, own_l(ph, pair), l_at(pair, vj), l_sem.at[pair, vj], partner)
        pltpu.make_async_copy(own_l(ph, pair), l_at(pair, vj), l_sem.at[pair, vj]).start()

    def l_arrived(cond, pair, j):
        arrived(cond, l_at(pair, j), l_sem.at[pair, j])

    def l_pass(cond, pair, j, there):
        send(cond, l_at(pair, j), l_at(pair, j), l_sem.at[pair, j], there)

    def l_relay_across(pair, j):
        l_arrived(mid, pair, j)
        l_pass(mid, pair, j, down)
        l_pass(mid, pair, j, partner)

    def l_share(cond, pair, j):
        l_arrived(cond, pair, j)
        l_pass(cond, pair, j, partner)

    TA, TR = pl.ds(0, 160), pl.ds(160, 144)
    own_near, own_far = both(cls, g_own == g_near), both(cls, g_own == g_far)

    def t_at(i, xs, rows):
        return tb.at[i, xs, rows], t_sem.at[i, xs, 0 if rows is TA else 1]

    def t_send(cond, i, xs, rows, theres):
        region, sem = t_at(i, xs, rows)
        copies = [pltpu.make_async_remote_copy(
            src_ref=region, dst_ref=region, send_sem=send_sem.at[len(pending)], recv_sem=sem,
            device_id=there, device_id_type=MESH) for there in theres]

        def work():
            for copy in copies:
                copy.start()

        when(cond, work)
        three = tb.at[0, pl.ds(0, 3), rows]
        pending.append((cond, pltpu.make_async_copy(three, three, send_sem.at[len(pending)]).wait))

    def t_arrived(cond, i, xs, rows):
        arrived(cond, *t_at(i, xs, rows))

    x_others, y_others = [dev_x(v) for v in (xp, xm, xf)], [dev_y(v) for v in (yp, ym, yf)]
    end_cls = both(end, cls)

    def t_start():
        for rows in (TA, TR):
            region, sem = t_at(yi, x, rows)
            send(both(end_cls, g_own == 0), t_in.at[rows], region, sem, border)
            send(both(end_cls, g_own == 1), t_in.at[rows], region, sem, behind)
            when(own_near, pltpu.make_async_copy(t_in.at[rows], region, sem).start)

    def t_own(cond):
        t_arrived(cond, yi, x, TA)
        t_send(cond, yi, x, TA, x_others)
        t_arrived(cond, yi, x, TR)
        t_send(cond, yi, x, TR, y_others)
        t_send(cond, yi, x, TR, x_others)
        t_send(cond, yi, x, TA, y_others)

    def t_second(g):
        for xs in cols_of(g, yi):
            t_arrived(both(cls, xs != x), yi, xs, TA)
            t_send(both(cls, xs != x), yi, xs, TA, y_others)
        i = row_of(g, x)
        cond = jnp.logical_or(non, i != yi)
        t_arrived(cond, i, x, TR)
        t_send(cond, i, x, TR, x_others)

    def t_join(g):
        for i in (0, 1):
            for xs in cols_of(g, i):
                t_arrived(jnp.logical_or(non, yi != i), i, xs, TA)
                t_arrived(xs != x, i, xs, TR)
            n, k = (g, 2 * g) if i == 0 else (3 - g, 2 * (1 - g))
            tn[n, 0:TB, :] = tb[i, k, 0:TB, :]
            tn[n, TB:V, :] = tb[i, k + 1, 0:TB, :]

    t_start()
    l_first()
    t_own(own_near)
    l_own(0)
    l_own(1)
    l_relay_across(0, j1)
    send(mid, own_l(1 - ph, 1), l_at(1, vj), l_sem.at[1, vj], up)
    l_share(end, 0, j1)
    l_share(mid, 0, je)
    t_own(own_far)
    t_second(g_near)
    l_relay_across(0, j2)
    l_share(end, 1, j1)
    l_relay_across(1, j1)
    l_share(end, 0, j2)
    l_share(mid, 1, je)
    t_second(g_far)
    l_relay_across(1, j2)
    l_share(end, 0, j3)
    t_join(g_near)
    partner_j = [2 * s + 1 - core for s in range(4)]
    l_arrived(None, 0, vj)
    for j in partner_j:
        l_arrived(None, 0, j)

    def lay(pair):
        rows = lr[pair].reshape(2, W, W)
        lk[pair, :, :W] = rows[0]
        lk[pair, :, W:] = rows[1]

    def first_half(pair, k, n):
        half = lax.dot_general(tn[n], lr[pair].reshape(2 * W, W), NT, preferred_element_type=F32).astype(BF)
        h[:W, k * W:(k + 1) * W] = half[:, :W]
        h[W:, k * W:(k + 1) * W] = half[:, W:]

    def join_halves(pair, g):
        first_half(pair, 0, g)
        first_half(pair, 1, 3 - g)

    def first(g):
        join_halves(0, g)
        acc[...] = jnp.dot(lk[0], h[...], preferred_element_type=F32)

    def second(g):
        total = acc[...] + jnp.dot(lk[1], h[...], preferred_element_type=F32)
        for k, c in ((0, g), (1, 1 - g)):
            block = total[:, k * W:(k + 1) * W].astype(BF)
            sb[k, 2 * c] = block[:SW]
            sb[k, 2 * c + 1] = block[SW:]

    lay(0)
    first(g_near)
    l_share(end, 1, j2)
    l_share(end, 1, j3)
    l_arrived(None, 1, vj)
    for j in partner_j:
        l_arrived(None, 1, j)

    @pl.when(end)
    def _():
        pl.semaphore_signal(line_sem, inc=1, device_id=border, device_id_type=MESH)

    lay(1)
    join_halves(1, g_near)
    second(g_near)

    A, B = pl.ds(0, 160), pl.ds(160, 160)

    def add(i, xs, rows, *others):
        total = sb[i, xs, rows, :].astype(F32)
        for other in others:
            total = total + other[...].astype(F32)
        return total

    def put(cond, i, xs, rows, *others):
        def work():
            sb[i, xs, rows, :] = add(i, xs, rows, *others).astype(BF)
        when(cond, work)

    def large(g):
        for slot, v in enumerate((xp, xm, xf)):
            i = row_of(g, v)
            send(None, sb.at[i, v, B], rxb.at[slot, i], rxb_sem.at[slot, i], dev_x(v))
        for k in range(2):
            xs = cols_of(g, 1 - yi)[k]
            send(cls, sb.at[1 - yi, xs, A], rya.at[2, xs], rya_sem.at[2, xs], dev_y(yf))
            xs = cols_of(g, ip)[k]
            send(non, sb.at[ip, xs, A], rya.at[0, xs], rya_sem.at[0, xs], dev_y(yp))
            xs = cols_of(g, im)[k]
            send(non, sb.at[im, xs, A], rya.at[1, xs], rya_sem.at[1, xs], dev_y(ym))

    def small(g):
        i = row_of(g, x)
        for slot in range(3):
            arrived(None, rxb.at[slot, i], rxb_sem.at[slot, i])
        put(None, i, x, B, rxb.at[0, i], rxb.at[1, i], rxb.at[2, i])
        send(both(cls, yi != i), sb.at[i, x, B], ryb.at[2], ryb_sem.at[2], dev_y(yf))
        send(both(non, ip == i), sb.at[i, x, B], ryb.at[0], ryb_sem.at[0], dev_y(yp))
        send(both(non, im == i), sb.at[i, x, B], ryb.at[1], ryb_sem.at[1], dev_y(ym))
        for xs in cols_of(g, yi):
            for slot in range(3):
                arrived(cls, rya.at[slot, xs], rya_sem.at[slot, xs])
            put(cls, yi, xs, A, rya.at[0, xs], rya.at[1, xs], rya.at[2, xs])
        for slot, v in enumerate((xp, xm, xf)):
            send(both(cls, row_of(g, v) == yi), sb.at[yi, v, A], rxa.at[slot], rxa_sem.at[slot], dev_x(v))

    large(g_near)
    t_join(g_far)
    first(g_far)
    join_halves(1, g_far)
    second(g_far)
    large(g_far)
    small(g_near)
    pl.semaphore_wait(line_sem, 1)

    @pl.when(end)
    def _():
        pl.semaphore_signal(line_sem, inc=1, device_id=up, device_id_type=MESH)

    small(g_far)
    for slot in range(3):
        arrived(cls, ryb.at[slot], ryb_sem.at[slot])
        arrived(cls, rxa.at[slot], rxa_sem.at[slot])

    @pl.when(cls)
    def _():
        fin[0:160, :] = add(yi, x, A, rxa.at[0], rxa.at[1], rxa.at[2])
        fin[160:320, :] = add(yi, x, B, ryb.at[0], ryb.at[1], ryb.at[2])
        fin[320:, :] = jnp.zeros((64, W), F32)
        zs[...] = fin[...].T.astype(BF).reshape(8, LW, 384)

    away = z_owner != zh
    z_first = jnp.where((zl < 2) == away, 0, 3)
    z_step = jnp.where(z_first == 0, 1, -1)
    for o in range(4):
        for k in (0, 1):
            j = (z_first + o * z_step) * 2 + k
            send(both(cls, jnp.logical_or(away, j != vj)), zs.at[j], zr.at[zl], z_sem.at[zl],
                 dev(z_owner * 16 + y * 4 + x, j))
    when(both(cls, z_owner == zh), pltpu.make_async_copy(zs.at[vj], zr.at[zl], z_sem.at[zl]).start)
    for s in range(4):
        arrived(None, zr.at[s], z_sem.at[s])
    total = zr[0].astype(F32) + zr[1].astype(F32) + zr[2].astype(F32) + zr[3].astype(F32)
    for q in range(4):
        out[:, q * LB:(q + 1) * LB] = total[:LB, q * LW:q * LW + LB]

    assert len(pending) <= N_SEND, len(pending)
    for cond, wait in pending:
        when(cond, wait)


def shards(amplitudes, chol_vectors):
    dma = pltpu.SemaphoreType.DMA
    vmem = pltpu.VMEM
    turned = pl.pallas_call(
        kernel,
        out_shape=jax.ShapeDtypeStruct((LB, TB), F32),
        in_specs=[pl.BlockSpec(memory_space=pltpu.VMEM)] * 2,
        out_specs=pl.BlockSpec(memory_space=pltpu.VMEM),
        scratch_shapes=[
            vmem((TW, W), BF), vmem((8, LW, W), BF),
            vmem((2, 2, 8, LW, W), BF), vmem((2, W, 2 * W), BF),
            vmem((2, 4, TW, W), BF), vmem((4, W, W), BF), vmem((2 * W, 2 * W), BF),
            vmem((W, 2 * W), F32), vmem((2, 4, SW, W), BF),
            vmem((3, 2, 160, W), BF), vmem((3, 4, 160, W), BF), vmem((3, 160, W), BF), vmem((3, 160, W), BF),
            vmem((384, W), F32), vmem((8, LW, 384), BF), vmem((4, LW, 384), BF),
            dma((N_SEND,)), dma((2, 8)), dma((2, 4, 2)),
            dma((3, 2)), dma((3, 4)), dma((3,)), dma((3,)), dma((4,)),
            pltpu.SemaphoreType.REGULAR,
        ],
        compiler_params=pltpu.CompilerParams(
            collective_id=0, has_side_effects=True, vmem_limit_bytes=52 << 20),
        name="ladder",
    )(amplitudes, chol_vectors)
    return turned.T


def solution(mesh):
    placed = (P("chol", None), P("chol", "virt", None))
    return jax.shard_map(
        shards, mesh=mesh, in_specs=placed, out_specs=P("chol", "virt"), check_vma=False
    )
```

time: 98.1 us -> 91.9 us (0.937); the launches traced: 96.8 us -> 91.8 us
  Pallas kernels: 94.9 us -> 89.9 us
    pallas_call x1, Pallas kernels: 94.9 us -> 89.9 us  [shards(): pl.pallas_call(kernel, out_shape=jax.ShapeDtypeStruct((LB, TB), F32), in_...]
where the time goes in v3:
time: 91.9 us; the launch traced here: 91.8 us
  Pallas kernels  89.9 us (98%)
  local copies, waits for them, and re-layouts  1.93 us (2%)
    pallas_call x1, Pallas kernels, shards(): pl.pallas_call(kernel, out_shape=jax.ShapeDtypeStruct((LB, TB), F32), in_...  89.9 us
    unnamed x4, local copies, waits for them, and re-layouts  1.93 us

profile of v3, /device:TPU:7, one launch (start us, length us, event | category | flops | bytes accessed | tf_op | source)
XLA Modules:
  0.0 91.8 jit_solution(16341147430403552647)
XLA Ops:
  0.0 0.0 copy-start
  0.0 1.3 %copy.3.l_raw = bf16[8,75,600]{2,1,0:T(8,128)(2,1)S(1)} copy(bf16[8,75,600]{2,0,1:T(8,128)(2,1)} %param.3) | data formatting | bytes 1440000 | tf_op args[1]
  1.3 0.0 copy-done
  1.3 89.9 %ladder.1 = f32[75,300]{1,0:T(8,128)S(1)} custom-call(bf16[300,600]{1,0:T(8,128)(2,1)S(1)} %copy-done, bf16[8,75,600]{2,1,0:T(8,128)(2,1)S(1)} %copy.3.l_raw), custom_call_target="tpu_custom_call" | custom-call | tf_op jit(solution)/shard_map/ladder/pallas_call | solution.py:357
  91.2 0.7 copy.5
Async XLA Ops:
  0.0 1.3 %copy-start = (bf16[300,600]{1,0:T(8,128)(2,1)S(1)}, bf16[300,600]{1,0:T(8,128)(2,1)}, u32[]{:S(2)}) copy-start(bf16[300,600]{1,0:T(8,128)(2,1)} %t_raw.1) | copy-start | bytes 1080004

commit v4 on v3

--- a/solution.py
+++ b/solution.py
@@ -12,7 +12,7 @@
 TB, TW = 300, 304
 LB, LW = 75, 80
 SW = 320
-N_SEND = 84
+N_SEND = 90
 
 
 def kernel(t_raw, l_raw, out, t_in, l_in, lr, lk, tb, tn, h, acc, sb,
@@ -164,7 +164,7 @@
     def t_arrived(cond, i, xs, rows):
         arrived(cond, *t_at(i, xs, rows))
 
-    x_others, y_others = [dev_x(v) for v in (xp, xm, xf)], [dev_y(v) for v in (yp, ym, yf)]
+    x_others, y_others = [dev_x(v) for v in (xf, xp, xm)], [dev_y(v) for v in (yf, yp, ym)]
     end_cls = both(end, cls)
 
     def t_start():
@@ -209,16 +209,16 @@
     send(mid, own_l(1 - ph, 1), l_at(1, vj), l_sem.at[1, vj], up)
     l_share(end, 0, j1)
     l_share(mid, 0, je)
+    t_second(g_near)
     t_own(own_far)
-    t_second(g_near)
     l_relay_across(0, j2)
     l_share(end, 1, j1)
     l_relay_across(1, j1)
     l_share(end, 0, j2)
     l_share(mid, 1, je)
-    t_second(g_far)
     l_relay_across(1, j2)
     l_share(end, 0, j3)
+    t_second(g_far)
     t_join(g_near)
     partner_j = [2 * s + 1 - core for s in range(4)]
     l_arrived(None, 0, vj)
@@ -243,12 +243,26 @@
         join_halves(0, g)
         acc[...] = jnp.dot(lk[0], h[...], preferred_element_type=F32)
 
+    A, B = pl.ds(0, 160), pl.ds(160, 160)
+
+    def large(g, part):
+        for slot, v in ((2, xf), (0, xp), (1, xm)):
+            i = row_of(g, v)
+            send(v % 2 == part, sb.at[i, v, B], rxb.at[slot, i], rxb_sem.at[slot, i], dev_x(v))
+        xs = cols_of(g, 1 - yi)[part]
+        send(cls, sb.at[1 - yi, xs, A], rya.at[2, xs], rya_sem.at[2, xs], dev_y(yf))
+        xs = cols_of(g, ip)[part]
+        send(non, sb.at[ip, xs, A], rya.at[0, xs], rya_sem.at[0, xs], dev_y(yp))
+        xs = cols_of(g, im)[part]
+        send(non, sb.at[im, xs, A], rya.at[1, xs], rya_sem.at[1, xs], dev_y(ym))
+
     def second(g):
-        total = acc[...] + jnp.dot(lk[1], h[...], preferred_element_type=F32)
-        for k, c in ((0, g), (1, 1 - g)):
-            block = total[:, k * W:(k + 1) * W].astype(BF)
-            sb[k, 2 * c] = block[:SW]
-            sb[k, 2 * c + 1] = block[SW:]
+        for part in (0, 1):
+            rows = slice(part * SW, (part + 1) * SW)
+            total = acc[rows, :] + jnp.dot(lk[1, rows, :], h[...], preferred_element_type=F32)
+            for k, c in ((0, g), (1, 1 - g)):
+                sb[k, 2 * c + part] = total[:, k * W:(k + 1) * W].astype(BF)
+            large(g, part)
 
     lay(0)
     first(g_near)
@@ -266,7 +280,6 @@
     join_halves(1, g_near)
     second(g_near)
 
-    A, B = pl.ds(0, 160), pl.ds(160, 160)
 
     def add(i, xs, rows, *others):
         total = sb[i, xs, rows, :].astype(F32)
@@ -278,18 +291,6 @@
         def work():
             sb[i, xs, rows, :] = add(i, xs, rows, *others).astype(BF)
         when(cond, work)
-
-    def large(g):
-        for slot, v in enumerate((xp, xm, xf)):
-            i = row_of(g, v)
-            send(None, sb.at[i, v, B], rxb.at[slot, i], rxb_sem.at[slot, i], dev_x(v))
-        for k in range(2):
-            xs = cols_of(g, 1 - yi)[k]
-            send(cls, sb.at[1 - yi, xs, A], rya.at[2, xs], rya_sem.at[2, xs], dev_y(yf))
-            xs = cols_of(g, ip)[k]
-            send(non, sb.at[ip, xs, A], rya.at[0, xs], rya_sem.at[0, xs], dev_y(yp))
-            xs = cols_of(g, im)[k]
-            send(non, sb.at[im, xs, A], rya.at[1, xs], rya_sem.at[1, xs], dev_y(ym))
 
     def small(g):
         i = row_of(g, x)
@@ -303,15 +304,13 @@
             for slot in range(3):
                 arrived(cls, rya.at[slot, xs], rya_sem.at[slot, xs])
             put(cls, yi, xs, A, rya.at[0, xs], rya.at[1, xs], rya.at[2, xs])
-        for slot, v in enumerate((xp, xm, xf)):
+        for slot, v in ((2, xf), (0, xp), (1, xm)):
             send(both(cls, row_of(g, v) == yi), sb.at[yi, v, A], rxa.at[slot], rxa_sem.at[slot], dev_x(v))
 
-    large(g_near)
     t_join(g_far)
     first(g_far)
     join_halves(1, g_far)
     second(g_far)
-    large(g_far)
     small(g_near)
     pl.semaphore_wait(line_sem, 1)
 

time: 91.9 us -> 87.4 us (0.951)
  Pallas kernels: 89.9 us -> 85.4 us
    pallas_call x1, Pallas kernels: 89.9 us -> 85.4 us  [shards(): pl.pallas_call(kernel, out_shape=jax.ShapeDtypeStruct((LB, TB), F32), in_...]
where the time goes in v4:
time: 87.4 us; the launch traced here: 87.3 us
  Pallas kernels  85.4 us (98%)
  local copies, waits for them, and re-layouts  1.93 us (2%)
    pallas_call x1, Pallas kernels, shards(): pl.pallas_call(kernel, out_shape=jax.ShapeDtypeStruct((LB, TB), F32), in_...  85.4 us
    unnamed x4, local copies, waits for them, and re-layouts  1.93 us

profile of v4, /device:TPU:7, one launch (start us, length us, event | category | flops | bytes accessed | tf_op | source)
XLA Modules:
  0.0 87.3 jit_solution(7050976979818720196)
XLA Ops:
  0.0 0.0 copy-start
  0.0 1.3 %copy.3.l_raw = bf16[8,75,600]{2,1,0:T(8,128)(2,1)S(1)} copy(bf16[8,75,600]{2,0,1:T(8,128)(2,1)} %param.3) | data formatting | bytes 1440000 | tf_op args[1]
  1.3 0.0 copy-done
  1.3 85.4 %ladder.1 = f32[75,300]{1,0:T(8,128)S(1)} custom-call(bf16[300,600]{1,0:T(8,128)(2,1)S(1)} %copy-done, bf16[8,75,600]{2,1,0:T(8,128)(2,1)S(1)} %copy.3.l_raw), custom_call_target="tpu_custom_call" | custom-call | tf_op jit(solution)/shard_map/ladder/pallas_call | solution.py:356
  86.7 0.7 copy.5
Async XLA Ops:
  0.0 1.3 %copy-start = (bf16[300,600]{1,0:T(8,128)(2,1)S(1)}, bf16[300,600]{1,0:T(8,128)(2,1)}, u32[]{:S(2)}) copy-start(bf16[300,600]{1,0:T(8,128)(2,1)} %t_raw.1) | copy-start | bytes 1080004

commit v5 on v4

--- a/solution.py
+++ b/solution.py
@@ -86,6 +86,7 @@
     l_in[:, :, V - 88:] = jnp.zeros((8, LW, W - V + 88), BF)
     l_in[:, :LB, :V] = l_raw[...]
     tn[:, V:, :] = jnp.zeros((4, W - V, W), BF)
+    fin[SW:, :] = jnp.zeros((64, W), BF)
     pl.semaphore_wait(barrier, 11)
 
     pending = []
@@ -325,10 +326,9 @@
 
     @pl.when(cls)
     def _():
-        fin[0:160, :] = add(yi, x, A, rxa.at[0], rxa.at[1], rxa.at[2])
-        fin[160:320, :] = add(yi, x, B, ryb.at[0], ryb.at[1], ryb.at[2])
-        fin[320:, :] = jnp.zeros((64, W), F32)
-        zs[...] = fin[...].T.astype(BF).reshape(8, LW, 384)
+        fin[0:160, :] = add(yi, x, A, rxa.at[0], rxa.at[1], rxa.at[2]).astype(BF)
+        fin[160:320, :] = add(yi, x, B, ryb.at[0], ryb.at[1], ryb.at[2]).astype(BF)
+        zs[...] = fin[...].T.reshape(8, LW, 384)
 
     away = z_owner != zh
     z_first = jnp.where((zl < 2) == away, 0, 3)
@@ -364,7 +364,7 @@
             vmem((2, 4, TW, W), BF), vmem((4, W, W), BF), vmem((2 * W, 2 * W), BF),
             vmem((W, 2 * W), F32), vmem((2, 4, SW, W), BF),
             vmem((3, 2, 160, W), BF), vmem((3, 4, 160, W), BF), vmem((3, 160, W), BF), vmem((3, 160, W), BF),
-            vmem((384, W), F32), vmem((8, LW, 384), BF), vmem((4, LW, 384), BF),
+            vmem((384, W), BF), vmem((8, LW, 384), BF), vmem((4, LW, 384), BF),
             dma((N_SEND,)), dma((2, 8)), dma((2, 4, 2)),
             dma((3, 2)), dma((3, 4)), dma((3,)), dma((3,)), dma((4,)),
             pltpu.SemaphoreType.REGULAR,

time: 87.4 us -> 87.4 us (level)
  no operation moved by 1% of the time
where the time goes in v5:
time: 87.4 us; the launch traced here: 87.3 us
  Pallas kernels  85.4 us (98%)
  local copies, waits for them, and re-layouts  1.93 us (2%)
    pallas_call x1, Pallas kernels, shards(): pl.pallas_call(kernel, out_shape=jax.ShapeDtypeStruct((LB, TB), F32), in_...  85.4 us
    unnamed x4, local copies, waits for them, and re-layouts  1.93 us

profile of v5, /device:TPU:7, one launch (start us, length us, event | category | flops | bytes accessed | tf_op | source)
XLA Modules:
  0.0 87.3 jit_solution(14947938621785982817)
XLA Ops:
  0.0 0.0 copy-start
  0.0 1.3 %copy.3.l_raw = bf16[8,75,600]{2,1,0:T(8,128)(2,1)S(1)} copy(bf16[8,75,600]{2,0,1:T(8,128)(2,1)} %param.3) | data formatting | bytes 1440000 | tf_op args[1]
  1.3 0.0 copy-done
  1.3 85.4 %ladder.1 = f32[75,300]{1,0:T(8,128)S(1)} custom-call(bf16[300,600]{1,0:T(8,128)(2,1)S(1)} %copy-done, bf16[8,75,600]{2,1,0:T(8,128)(2,1)S(1)} %copy.3.l_raw), custom_call_target="tpu_custom_call" | custom-call | tf_op jit(solution)/shard_map/ladder/pallas_call | solution.py:356
  86.7 0.7 copy.5
Async XLA Ops:
  0.0 1.3 %copy-start = (bf16[300,600]{1,0:T(8,128)(2,1)S(1)}, bf16[300,600]{1,0:T(8,128)(2,1)}, u32[]{:S(2)}) copy-start(bf16[300,600]{1,0:T(8,128)(2,1)} %t_raw.1) | copy-start | bytes 1080004
